TPU v7x, 32 devices: a whole 2x2x4 slice. The times are simulated.
32 devices in a mesh: rows: 8 (over z, x), ka: 4 (over y, core).
Axes of the slice: x: 2, y: 2, z: 4, core: 2. Of those that a mesh axis runs over, the one named last changes fastest.
Arguments:
- pair_repr: bfloat16 [512, 512, 128], P('rows', 'ka'), may hold values from -6 to 6
- pair_mask: int32 [512, 512], P('rows', 'ka'), may hold values 0 or 1
- ln_gain: float32 [128], replicated, may hold values from 0.1 to 1.9
- ln_bias: float32 [128], replicated, may hold values from -3 to 3
- w_proj: bfloat16 [128, 256], replicated, may hold values from -0.5 to 0.5
- w_gate: bfloat16 [128, 256], replicated, may hold values from -0.5 to 0.5
- w_out_gate: bfloat16 [128, 128], replicated, may hold values from -0.5 to 0.5
- out_gain: float32 [128], replicated, may hold values from 0.1 to 1.9
- out_bias: float32 [128], replicated, may hold values from -3 to 3
- w_out: bfloat16 [128, 128], replicated, may hold values from -0.5 to 0.5
Outputs:
- update: bfloat16 [512, 512, 128], P('rows', 'ka')
All inputs are finite; a program needn't handle non-finite values. No bound on the sum of `pair_mask` on one device may be relied on, other than what follows from the above.
Results may differ from a plain program's by a relative error of at most 0.015.
Values may be sent and summed in bfloat16 or wider, within the bound.
No kernel may reach another device: no remote copies, remote signals or barrier semaphores. Data moves between devices by JAX's collectives and lax.ppermute only.
A program may use at most 64 MiB of HBM per device.

v0:
```python
import jax
import jax.numpy as jnp
from jax import lax
from jax.sharding import PartitionSpec as P


def layer_norm(values, gain_vec, bias_vec):
    center = jnp.mean(values, axis=-1, keepdims=True)
    deviate = values - center
    spread = jnp.mean(deviate * deviate, axis=-1, keepdims=True)
    return deviate * lax.rsqrt(spread + 1e-05) * gain_vec + bias_vec


def panel_sums(left_edge, right_edge):
    return jnp.einsum(
        "ikh,jkh->ijh",
        left_edge,
        lax.all_gather(right_edge, "rows", axis=0, tiled=True),
        preferred_element_type=jnp.float32,
    )


def body(
    pair_repr, pair_mask, ln_gain, ln_bias, w_proj, w_gate, w_out_gate, out_gain, out_bias, w_out
):
    row_count, col_count, chans = pair_repr.shape
    hidden = w_out.shape[0]
    normed = layer_norm(pair_repr.astype(jnp.float32), ln_gain, ln_bias).astype(jnp.bfloat16)
    flat_rows = normed.reshape(row_count * col_count, chans)
    projected = jnp.dot(flat_rows, w_proj, preferred_element_type=jnp.float32)
    gate_logits = jnp.dot(flat_rows, w_gate, preferred_element_type=jnp.float32)
    mask_col = pair_mask.reshape(row_count * col_count, 1).astype(jnp.float32)
    edges = (jax.nn.sigmoid(gate_logits) * projected * mask_col).astype(jnp.bfloat16)
    edges = edges.reshape(row_count, col_count, 2 * hidden)
    left_edge = edges[:, :, :hidden]
    right_edge = edges[:, :, hidden:]
    partial_sums = panel_sums(left_edge, right_edge)
    triangle = lax.psum_scatter(
        partial_sums.astype(jnp.bfloat16), "ka", scatter_dimension=1, tiled=True
    ).astype(jnp.float32)
    tri_normed = layer_norm(triangle, out_gain, out_bias).astype(jnp.bfloat16)
    out_gate = jax.nn.sigmoid(jnp.dot(flat_rows, w_out_gate, preferred_element_type=jnp.float32))
    projected_out = jnp.dot(
        tri_normed.reshape(row_count * col_count, hidden), w_out, preferred_element_type=jnp.float32
    )
    return (out_gate * projected_out).astype(jnp.bfloat16).reshape(row_count, col_count, chans)


def solution(mesh):
    placed = (P("rows", "ka", None), P("rows", "ka"), P(), P(), P(), P(), P(), P(), P(), P())
    return jax.shard_map(
        body, mesh=mesh, in_specs=placed, out_specs=P("rows", "ka", None), check_vma=False
    )
```

profile of v0, /device:TPU:0, one launch (start us, length us, event | category | flops | bytes accessed | tf_op | source)
XLA Modules:
  0.0 410.2 jit_solution(3869477217058959746)
XLA Ops:
  6.5 0.0 all-gather.2.cloned.1.call-start
  6.6 2.4 convert_reduce_fusion.1
  9.0 3.6 fusion.17
  12.6 2.5 fusion.20
  15.2 2.3 fusion.8
  17.5 3.6 fusion.3
  21.2 2.5 fusion.23
  23.7 2.9 copy.17
  26.6 0.2 reduce-scatter.4.cloned.1.call-start
  26.9 3.3 copy.18
  30.2 226.6 %all-gather.2.cloned.1.call-done = bf16[512,128,128]{1,0,2:T(8,128)(2,1)} async-done(((bf16[64,128,128]{1,0,2:T(8,128)(2,1)}), bf16[512,128,128]{1,0,2:T(8,128)(2,1)}) %all-gather.2.cloned.1.call-update) | async-done | bytes 16777232 | tf_op jit(solution)/shard_map/all_gather | solution.py:18
  256.7 11.4 %convert_bitcast_fusion = bf16[64,512,128]{1,0,2:T(8,128)(2,1)} fusion(bf16[512,128,128]{1,0,2:T(8,128)(2,1)} %all-gather.2.cloned.1.call-done, bf16[64,128,128]{1,0,2:T(8,128)(2,1)S(1)} %copy.18), kind=kOutput, calls=%fused_computation.13 | convolution fusion | flops 1077936128 | bytes 27262976 | tf_op jit(solution)/shard_map/ikh,jkh->ijh/dot_general | solution.py:15
  268.2 23.9 %copy.15 = bf16[64,512,128]{0,2,1:T(8,128)(2,1)} copy(bf16[64,512,128]{1,0,2:T(8,128)(2,1)} %convert_bitcast_fusion) | data formatting | bytes 16777216
  292.1 22.6 %reshape.53 = bf16[512,8192]{1,0:T(8,128)(2,1)} reshape(bf16[512,128,64]{2,1,0:T(8,128)(2,1)} %bitcast.25) | data formatting | bytes 16777216
  314.7 1.6 copy-done.4
  316.3 3.3 fusion.7
  319.6 64.9 %reduce-scatter.4.cloned.1.call-done = bf16[128,8192]{1,0:T(8,128)(2,1)} async-done(((bf16[512,8192]{1,0:T(8,128)(2,1)}), bf16[128,8192]{1,0:T(8,128)(2,1)}) %reduce-scatter.4.cloned.1.call-update) | async-done | bytes 2097168
  384.4 6.9 %reshape.54 = bf16[128,128,64]{2,1,0:T(8,128)(2,1)} reshape(bf16[128,8192]{1,0:T(8,128)(2,1)} %reduce-scatter.4.cloned.1.call-done) | data formatting | bytes 4194304
  391.4 5.9 %copy.16 = bf16[64,128,128]{1,0,2:T(8,128)(2,1)S(1)} copy(bf16[64,128,128]{0,2,1:T(8,128)(2,1)} %bitcast.30) | data formatting | bytes 4194304
  397.3 0.4 convert_reduce_fusion
  397.6 0.6 fusion.13
  398.3 0.9 fusion.16
  399.2 0.3 copy-done.5
  399.5 3.9 fusion.6
  (33 shorter events, 0.1 us)
Async XLA Ops:
  6.5 8.6 %copy-start = (bf16[128,256]{1,0:T(8,128)(2,1)S(1)}, bf16[128,256]{1,0:T(8,128)(2,1)}, u32[]{:S(2)}) copy-start(bf16[128,256]{1,0:T(8,128)(2,1)} %param.15) | copy-start | bytes 196612
  6.5 6.1 %copy-start.2 = (bf16[64,128,128]{2,1,0:T(8,128)(2,1)S(1)}, bf16[64,128,128]{2,1,0:T(8,128)(2,1)}, u32[]{:S(2)}) copy-start(bf16[64,128,128]{2,1,0:T(8,128)(2,1)} %param.10) | copy-start | bytes 6291460
  6.5 6.0 %copy-start.8 = (s32[64,128]{1,0:T(8,128)S(1)}, s32[64,128]{1,0:T(8,128)}, u32[]{:S(2)}) copy-start(s32[64,128]{1,0:T(8,128)} %param.11) | copy-start | bytes 98308
  6.5 6.1 %copy-start.10 = (f32[128]{0:T(128)S(1)}, f32[128]{0:T(128)}, u32[]{:S(2)}) copy-start(f32[128]{0:T(128)} %param.12) | copy-start | bytes 1540
  6.5 6.1 %copy-start.9 = (f32[128]{0:T(128)S(1)}, f32[128]{0:T(128)}, u32[]{:S(2)}) copy-start(f32[128]{0:T(128)} %param.13) | copy-start | bytes 1540
  6.5 250.2 %all-gather.2.cloned.1.call-start = ((), (), s32[]{:S(2)}) async-start(), calls=%async_computation.1 | async-start | bytes 18874368 | tf_op jit(solution)/shard_map/all_gather | solution.py:18
  15.1 2.4 copy-start.3
  15.2 2.4 copy-start.6
  26.6 357.8 %reduce-scatter.4.cloned.1.call-start = ((), (), s32[]{:S(2)}) async-start(), calls=%async_computation.2 | async-start | bytes 10485760
  314.7 1.6 copy-start.4
  314.7 1.6 copy-start.13
  391.4 6.9 %copy-start.11 = (f32[128]{0:T(128)S(1)}, f32[128]{0:T(128)}, u32[]{:S(2)}) copy-start(f32[128]{0:T(128)} %param.18) | copy-start | bytes 1540
  391.4 6.9 %copy-start.12 = (f32[128]{0:T(128)S(1)}, f32[128]{0:T(128)}, u32[]{:S(2)}) copy-start(f32[128]{0:T(128)} %param.17) | copy-start | bytes 1540
  397.3 2.2 copy-start.5
  397.3 2.2 copy-start.7
  399.1 4.2 %copy-start.1 = (bf16[128,256]{1,0:T(8,128)(2,1)S(1)}, bf16[128,256]{1,0:T(8,128)(2,1)}, u32[]{:S(2)}) copy-start(bf16[128,256]{1,0:T(8,128)(2,1)} %param.15) | copy-start | bytes 196612
Sparse Core Ops, SparseCore 0:
  26.7 229.9 all-gather.1
  314.8 69.5 reduce-scatter.3
where the time goes:
time: 412 us; the launch traced here: 410 us
  waiting for transfers between devices  291 us (71%)
  local copies, waits for them, and re-layouts  69.9 us (17%)
  matrix products  24.6 us (6%)
  between operations  13.6 us (3%)
  other arithmetic  10.3 us (2%)
    all_gather x1, waiting for transfers between devices, panel_sums(): lax.all_gather(right_edge, 'rows', axis=0, tiled=True)  227 us
    unnamed x34, local copies, waits for them, and re-layouts  67.4 us
    unnamed x3, waiting for transfers between devices  64.9 us
    dot_general x1, matrix products, panel_sums(): jnp.einsum('ikh,jkh->ijh', left_edge, lax.all_gather(right_edge, 'rows',...  11.4 us
  transfers between devices with their start and end apart: 2, of which 2 were waited for; matrix products, arithmetic and copies ran while one was open for 2% of the time, Pallas kernels for 0%

commit v1 on v0

v1 whole, which is shorter than its diff:
```python
import jax
import jax.numpy as jnp
from jax import lax
from jax.experimental import pallas as pl
from jax.experimental.pallas import tpu as pltpu
from jax.sharding import PartitionSpec as P

EPS = 1e-05
F32 = jnp.float32
BF16 = jnp.bfloat16


def sigmoid(x):
    return 0.5 * jnp.tanh(0.5 * x) + 0.5


def layer_norm(values, gain_vec, bias_vec):
    center = jnp.mean(values, axis=-1, keepdims=True)
    deviate = values - center
    spread = jnp.mean(deviate * deviate, axis=-1, keepdims=True)
    return deviate * lax.rsqrt(spread + EPS) * gain_vec + bias_vec


def contract(a, b, dim_a, dim_b):
    return lax.dot_general(a, b, (((dim_a,), (dim_b,)), ((), ())), preferred_element_type=F32)


def edge_kernel(z_ref, m_ref, gain_ref, bias_ref, wp_ref, wg_ref, out_ref):
    rows, cols, chans = z_ref.shape
    dests, sides, each, _, _ = out_ref.shape
    wp = wp_ref[...]
    wg = wg_ref[...]
    mask = m_ref[...].astype(F32)
    edges = []
    for i in range(rows):
        normed = layer_norm(z_ref[i].astype(F32), gain_ref[...], bias_ref[...]).astype(BF16)
        proj = contract(wp, normed, 0, 1)
        gate = contract(wg, normed, 0, 1)
        edges.append(sigmoid(gate) * proj * mask[i : i + 1, :])
    by_h = jnp.swapaxes(jnp.stack(edges, axis=0), 0, 1).astype(BF16)
    by_h = by_h.reshape(sides, dests, each, rows, cols)
    for s in range(sides):
        out_ref[:, s] = by_h[s]


def gate_kernel(z_ref, gain_ref, bias_ref, w_ref, out_ref):
    rows, cols, chans = z_ref.shape
    flat = z_ref[...].astype(F32).reshape(rows * cols, chans)
    normed = layer_norm(flat, gain_ref[...], bias_ref[...]).astype(BF16)
    gate = sigmoid(contract(normed, w_ref[...], 1, 0))
    out_ref[...] = gate.astype(BF16).reshape(rows, cols, chans)


def make_triangle_kernel(row_parts, col_parts):
    def triangle_kernel(e_ref, out_ref):
        def whole(side):
            return jnp.concatenate(
                [
                    jnp.concatenate(
                        [e_ref[r * col_parts + c, side, 0] for c in range(col_parts)], axis=1
                    )
                    for r in range(row_parts)
                ],
                axis=0,
            )

        tri = contract(whole(0), whole(1), 1, 1).astype(BF16)
        bi = tri.shape[0] // row_parts
        bj = tri.shape[1] // col_parts
        for r in range(row_parts):
            for c in range(col_parts):
                out_ref[r * col_parts + c, 0] = tri[r * bi : (r + 1) * bi, c * bj : (c + 1) * bj]

    return triangle_kernel


def out_kernel(t_ref, g_ref, gain_ref, bias_ref, w_ref, out_ref):
    tri = t_ref[...].astype(F32)
    deviate = tri - jnp.mean(tri, axis=0, keepdims=True)
    spread = jnp.mean(deviate * deviate, axis=0, keepdims=True)
    scaled = jnp.swapaxes(deviate * lax.rsqrt(spread + EPS), 0, 1)
    w = w_ref[...]
    for i in range(scaled.shape[0]):
        normed = (scaled[i] * gain_ref[...] + bias_ref[...]).astype(BF16)
        update = contract(normed, w, 0, 0)
        out_ref[i] = (g_ref[i].astype(F32) * update).astype(BF16)


def whole_spec(array):
    return pl.BlockSpec(array.shape, lambda *_: (0,) * array.ndim)


def make_channel_body(row_parts, col_parts):
    parts = row_parts * col_parts
    axes = ("rows", "ka")

    def body(z, mask, ln_gain, ln_bias, w_proj, w_gate, w_out_gate, out_gain, out_bias, w_out):
        rows, cols, chans = z.shape
        hidden = w_out.shape[0]
        each = hidden // parts
        step = min(16, rows)
        gain_row = ln_gain.reshape(1, chans)
        bias_row = ln_bias.reshape(1, chans)
        par = pltpu.CompilerParams(dimension_semantics=("arbitrary",))
        z_spec = pl.BlockSpec((step, cols, chans), lambda i: (i, 0, 0))
        edges = pl.pallas_call(
            edge_kernel,
            grid=(rows // step,),
            in_specs=[
                z_spec,
                pl.BlockSpec((step, cols), lambda i: (i, 0)),
                whole_spec(gain_row),
                whole_spec(bias_row),
                whole_spec(w_proj),
                whole_spec(w_gate),
            ],
            out_specs=pl.BlockSpec((parts, 2, each, step, cols), lambda i: (0, 0, 0, i, 0)),
            out_shape=jax.ShapeDtypeStruct((parts, 2, each, rows, cols), BF16),
            compiler_params=par,
            name="edges",
        )(z, mask, gain_row, bias_row, w_proj, w_gate)
        mine = lax.all_to_all(edges, axes, 0, 0, tiled=True)
        out_gate = pl.pallas_call(
            gate_kernel,
            grid=(rows // step,),
            in_specs=[z_spec, whole_spec(gain_row), whole_spec(bias_row), whole_spec(w_out_gate)],
            out_specs=z_spec,
            out_shape=jax.ShapeDtypeStruct((rows, cols, chans), BF16),
            compiler_params=par,
            name="out_gate",
        )(z, gain_row, bias_row, w_out_gate)
        sums = pl.pallas_call(
            make_triangle_kernel(row_parts, col_parts),
            grid=(each,),
            in_specs=[pl.BlockSpec((parts, 2, 1, rows, cols), lambda h: (0, 0, h, 0, 0))],
            out_specs=pl.BlockSpec((parts, 1, rows, cols), lambda h: (0, h, 0, 0)),
            out_shape=jax.ShapeDtypeStruct((parts, each, rows, cols), BF16),
            compiler_params=par,
            name="triangle",
        )(mine)
        tri = lax.all_to_all(sums, axes, 0, 0, tiled=True).reshape(hidden, rows, cols)
        gain_wide = jnp.broadcast_to(out_gain.reshape(hidden, 1), (hidden, cols))
        bias_wide = jnp.broadcast_to(out_bias.reshape(hidden, 1), (hidden, cols))
        return pl.pallas_call(
            out_kernel,
            grid=(rows // step,),
            in_specs=[
                pl.BlockSpec((hidden, step, cols), lambda i: (0, i, 0)),
                z_spec,
                whole_spec(gain_wide),
                whole_spec(bias_wide),
                whole_spec(w_out),
            ],
            out_specs=z_spec,
            out_shape=jax.ShapeDtypeStruct((rows, cols, chans), BF16),
            compiler_params=par,
            name="update",
        )(tri, out_gate, gain_wide, bias_wide, w_out)

    return body


def gathered_body(z, mask, ln_gain, ln_bias, w_proj, w_gate, w_out_gate, out_gain, out_bias, w_out):
    rows, cols, chans = z.shape
    hidden = w_out.shape[0]
    normed = layer_norm(z.astype(F32), ln_gain, ln_bias).astype(BF16)
    flat = normed.reshape(rows * cols, chans)
    projected = jnp.dot(flat, w_proj, preferred_element_type=F32)
    gate_logits = jnp.dot(flat, w_gate, preferred_element_type=F32)
    mask_col = mask.reshape(rows * cols, 1).astype(F32)
    edges = (jax.nn.sigmoid(gate_logits) * projected * mask_col).astype(BF16)
    edges = edges.reshape(rows, cols, 2 * hidden)
    partial_sums = jnp.einsum(
        "ikh,jkh->ijh",
        edges[:, :, :hidden],
        lax.all_gather(edges[:, :, hidden:], "rows", axis=0, tiled=True),
        preferred_element_type=F32,
    )
    triangle = lax.psum_scatter(
        partial_sums.astype(BF16), "ka", scatter_dimension=1, tiled=True
    ).astype(F32)
    tri_normed = layer_norm(triangle, out_gain, out_bias).astype(BF16)
    out_gate = jax.nn.sigmoid(jnp.dot(flat, w_out_gate, preferred_element_type=F32))
    projected_out = jnp.dot(
        tri_normed.reshape(rows * cols, hidden), w_out, preferred_element_type=F32
    )
    return (out_gate * projected_out).astype(BF16).reshape(rows, cols, chans)


def solution(mesh):
    row_parts, col_parts = mesh.shape["rows"], mesh.shape["ka"]
    channel_body = make_channel_body(row_parts, col_parts)

    def body(*args):
        hidden = args[-1].shape[0]
        if hidden % (row_parts * col_parts) == 0:
            return channel_body(*args)
        return gathered_body(*args)

    placed = (P("rows", "ka", None), P("rows", "ka"), P(), P(), P(), P(), P(), P(), P(), P())
    return jax.shard_map(
        body, mesh=mesh, in_specs=placed, out_specs=P("rows", "ka", None), check_vma=False
    )
```

time: 412 us -> 177 us (0.43)
  waiting for transfers between devices: 291 us -> 43 us
  blocking collectives: 0 us -> 101 us
  local copies, waits for them, and re-layouts: 69.9 us -> 1.52 us
  Pallas kernels: 0 us -> 27.6 us
  matrix products: 24.6 us -> 0 us
  between operations: 13.6 us -> 0.03 us
  other arithmetic: 10.3 us -> 0 us
    all_gather x1 -> x0, waiting for transfers between devices: 227 us -> none  [panel_sums(): lax.all_gather(right_edge, 'rows', axis=0, tiled=True)]
    all_to_all x0 -> x1, blocking collectives: none -> 101 us  [body(): mine = lax.all_to_all(edges, axes, 0, 0, tiled=True)]
    unnamed x34 -> x6, local copies, waits for them, and re-layouts: 67.4 us -> 0.02 us
    unnamed x3 -> x0, waiting for transfers between devices: 64.9 us -> none
    all_to_all x0 -> x1, waiting for transfers between devices: none -> 43 us  [body(): lax.all_to_all(sums, axes, 0, 0, tiled=True).reshape(hidden, rows, cols)]
    pallas_call x0 -> x4, Pallas kernels: none -> 27.6 us  [the longest x1 10.4 us: body(): pl.pallas_call(edge_kernel, grid=(rows // step,), in_specs=[z_spec, pl.Bl...]
    dot_general x5 -> x0, matrix products: 24.6 us -> none  [the longest x1 11.4 us: panel_sums(): jnp.einsum('ikh,jkh->ijh', left_edge, lax.all_gather(right_edge, 'rows',...]
    reduce_sum x4 -> x0, other arithmetic: 6.89 us -> none  [the longest x2 4.17 us: layer_norm(): spread = jnp.mean(deviate * deviate, axis=-1, keepdims=True)]
  transfers between devices with their start and end apart: 2 -> 1, of which waited for: 2 -> 1; matrix products, arithmetic and copies ran while one was open for 2% -> 0% of each run, Pallas kernels for 0% -> 3%
where the time goes in v1:
time: 177 us
  blocking collectives  101 us (57%)
  waiting for transfers between devices  43 us (24%)
  Pallas kernels  27.6 us (16%)
  starting transfers between devices  3.66 us (2%)
    all_to_all x1, blocking collectives, body(): mine = lax.all_to_all(edges, axes, 0, 0, tiled=True)  101 us
    all_to_all x1, waiting for transfers between devices, body(): lax.all_to_all(sums, axes, 0, 0, tiled=True).reshape(hidden, rows, cols)  43 us
    pallas_call x1, Pallas kernels, body(): pl.pallas_call(edge_kernel, grid=(rows // step,), in_specs=[z_spec, pl.Bl...  10.4 us
    pallas_call x1, Pallas kernels, body(): pl.pallas_call(out_kernel, grid=(rows // step,), in_specs=[pl.BlockSpec((...  6.47 us
    pallas_call x1, Pallas kernels, body(): pl.pallas_call(gate_kernel, grid=(rows // step,), in_specs=[z_spec, whole...  5.66 us
    pallas_call x1, Pallas kernels, body(): pl.pallas_call(make_triangle_kernel(row_parts, col_parts), grid=(each,),...  5.07 us
    all_to_all x1, starting transfers between devices, body(): lax.all_to_all(sums, axes, 0, 0, tiled=True).reshape(hidden, rows, cols)  3.66 us
  transfers between devices with their start and end apart: 1, of which 1 were waited for; matrix products, arithmetic and copies ran while one was open for 0% of the time, Pallas kernels for 3%

profile of v1, /device:TPU:0, one launch (start us, length us, event | category | flops | bytes accessed | tf_op | source)
XLA Modules:
  0.0 176.9 jit_solution(3902195872150262414)
XLA Ops:
  0.0 10.4 %edges.1 = bf16[32,2,4,64,128]{4,3,2,1,0:T(8,128)(2,1)} custom-call(bf16[64,128,128]{2,1,0:T(8,128)(2,1)} %z_ref.3, s32[64,128]{1,0:T(8,128)} %m_ref.1, f32[1,128]{1,0:T(1,128)} %bitcast.4, f32[1,128]{1,0:T(1,128)} %bitcast.6, bf16[128,256]{1,0:T(8,128)(2,1)} %wp_ref.1, bf16[128,256]{1,0:T(8,128)(2,1)} %wg_ref.1), custom_call_target="tpu_custom_call" | custom-call | tf_op jit(solution)/shard_map/edges/pallas_call | solution.py:106
  10.4 101.1 %all_to_all.10.e_ref = bf16[32,2,4,64,128]{4,3,2,1,0:T(8,128)(2,1)} all-to-all(bf16[32,2,4,64,128]{4,3,2,1,0:T(8,128)(2,1)} %edges.1), channel_id=1, replica_groups=mesh['rows'=8,'ka'=4] {'rows','ka'}, dimensions={0} | all-to-all | bytes 8388608 | tf_op jit(solution)/shard_map/all_to_all | solution.py:122
  111.5 5.1 %triangle.1 = bf16[32,4,64,128]{3,2,1,0:T(8,128)(2,1)} custom-call(bf16[32,2,4,64,128]{4,3,2,1,0:T(8,128)(2,1)} %all_to_all.10.e_ref), custom_call_target="tpu_custom_call" | custom-call | tf_op jit(solution)/shard_map/triangle/pallas_call | solution.py:132
  116.6 3.7 %all-to-all-start.1 = ((bf16[32,4,64,128]{3,2,1,0:T(8,128)(2,1)}), bf16[32,4,64,128]{3,2,1,0:T(8,128)(2,1)S(1)}, u32[]{:S(2)}, u32[]{:S(2)}) async-start(bf16[32,4,64,128]{3,2,1,0:T(8,128)(2,1)} %triangle.1), calls=%async_computation.1 | async-start | bytes 4194304 | tf_op jit(solution)/shard_map/all_to_all | solution.py:141
  120.2 0.0 copy-start.1
  120.2 0.0 copy-start.2
  120.3 5.7 %out_gate.1.g_ref = bf16[64,128,128]{2,1,0:T(8,128)(2,1)} custom-call(bf16[64,128,128]{2,1,0:T(8,128)(2,1)} %z_ref.3, f32[1,128]{1,0:T(1,128)} %bitcast.5, f32[1,128]{1,0:T(1,128)} %bitcast.7, bf16[128,128]{1,0:T(8,128)(2,1)} %w_ref.2), custom_call_target="tpu_custom_call" | custom-call | tf_op jit(solution)/shard_map/out_gate/pallas_call | solution.py:123
  125.9 43.0 %all-to-all-done.1 = bf16[32,4,64,128]{3,2,1,0:T(8,128)(2,1)S(1)} async-done(((bf16[32,4,64,128]{3,2,1,0:T(8,128)(2,1)}), bf16[32,4,64,128]{3,2,1,0:T(8,128)(2,1)S(1)}, u32[]{:S(2)}, u32[]{:S(2)}) %all-to-all-start.1) | async-done | bytes 2097184 | tf_op jit(solution)/shard_map/all_to_all | solution.py:141
  169.0 0.0 copy-start
  169.0 0.0 copy-done.1
  169.0 0.8 broadcast_in_dim.4.gain_ref
  169.8 0.0 copy-done.2
  169.8 0.7 broadcast_in_dim.5.bias_ref
  170.5 0.0 copy-done
  170.5 6.5 %update.1 = bf16[64,128,128]{2,1,0:T(8,128)(2,1)} custom-call(bf16[128,64,128]{2,1,0:T(8,128)(2,1)} %bitcast.3, bf16[64,128,128]{2,1,0:T(8,128)(2,1)} %out_gate.1.g_ref, f32[128,128]{1,0:T(8,128)} %broadcast_in_dim.4.gain_ref, f32[128,128]{1,0:T(8,128)} %broadcast_in_dim.5.bias_ref, bf16[128,128]{1,0:T(8,128)(2,1)} %w_ref.3), custom_call_target="tpu_custom_call" | custom-call | tf_op jit(solution)/shard_map/update/pallas_call | solution.py:144
Async XLA Ops:
  116.6 52.4 %all-to-all-start.1 = ((bf16[32,4,64,128]{3,2,1,0:T(8,128)(2,1)}), bf16[32,4,64,128]{3,2,1,0:T(8,128)(2,1)S(1)}, u32[]{:S(2)}, u32[]{:S(2)}) async-start(bf16[32,4,64,128]{3,2,1,0:T(8,128)(2,1)} %triangle.1), calls=%async_computation.1 | async-start | bytes 4194304 | tf_op jit(solution)/shard_map/all_to_all | solution.py:141
  120.2 48.7 %copy-start.1 = (f32[128]{0:T(128)S(1)}, f32[128]{0:T(128)}, u32[]{:S(2)}) copy-start(f32[128]{0:T(128)} %param.17) | copy-start | bytes 1540
  120.2 49.5 %copy-start.2 = (f32[128]{0:T(128)S(1)}, f32[128]{0:T(128)}, u32[]{:S(2)}) copy-start(f32[128]{0:T(128)} %param.18) | copy-start | bytes 1540
  169.0 1.5 copy-start

commit v2 on v1

--- a/solution.py
+++ b/solution.py
@@ -25,18 +25,28 @@
     return lax.dot_general(a, b, (((dim_a,), (dim_b,)), ((), ())), preferred_element_type=F32)
 
 
+def row_norm(z, gain_row, bias_row):
+    chans = z.shape[-1]
+    ones = jnp.ones((chans, chans), BF16)
+    deviate = z.astype(F32) - contract(z, ones, 1, 0) * (1.0 / chans)
+    square = deviate * deviate
+    high = square.astype(BF16)
+    low = (square - high.astype(F32)).astype(BF16)
+    spread = (contract(high, ones, 1, 0) + contract(low, ones, 1, 0)) * (1.0 / chans)
+    return (deviate * lax.rsqrt(spread + EPS) * gain_row + bias_row).astype(BF16)
+
+
 def edge_kernel(z_ref, m_ref, gain_ref, bias_ref, wp_ref, wg_ref, out_ref):
     rows, cols, chans = z_ref.shape
     dests, sides, each, _, _ = out_ref.shape
-    wp = wp_ref[...]
-    wg = wg_ref[...]
+    both = jnp.concatenate([wp_ref[...].T, wg_ref[...].T], axis=0)
     mask = m_ref[...].astype(F32)
+    flat = row_norm(z_ref[...].reshape(rows * cols, chans), gain_ref[...], bias_ref[...])
+    width = sides * dests * each
     edges = []
     for i in range(rows):
-        normed = layer_norm(z_ref[i].astype(F32), gain_ref[...], bias_ref[...]).astype(BF16)
-        proj = contract(wp, normed, 0, 1)
-        gate = contract(wg, normed, 0, 1)
-        edges.append(sigmoid(gate) * proj * mask[i : i + 1, :])
+        made = contract(both, flat[i * cols : (i + 1) * cols], 1, 1)
+        edges.append(sigmoid(made[width:]) * made[:width] * mask[i : i + 1, :])
     by_h = jnp.swapaxes(jnp.stack(edges, axis=0), 0, 1).astype(BF16)
     by_h = by_h.reshape(sides, dests, each, rows, cols)
     for s in range(sides):
@@ -45,9 +55,8 @@
 
 def gate_kernel(z_ref, gain_ref, bias_ref, w_ref, out_ref):
     rows, cols, chans = z_ref.shape
-    flat = z_ref[...].astype(F32).reshape(rows * cols, chans)
-    normed = layer_norm(flat, gain_ref[...], bias_ref[...]).astype(BF16)
-    gate = sigmoid(contract(normed, w_ref[...], 1, 0))
+    flat = row_norm(z_ref[...].reshape(rows * cols, chans), gain_ref[...], bias_ref[...])
+    gate = sigmoid(contract(flat, w_ref[...], 1, 0))
     out_ref[...] = gate.astype(BF16).reshape(rows, cols, chans)
 
 
@@ -80,8 +89,11 @@
     spread = jnp.mean(deviate * deviate, axis=0, keepdims=True)
     scaled = jnp.swapaxes(deviate * lax.rsqrt(spread + EPS), 0, 1)
     w = w_ref[...]
+    hidden, cols = scaled.shape[1:]
+    gain = jnp.broadcast_to(gain_ref[...], (cols, hidden)).T
+    bias = jnp.broadcast_to(bias_ref[...], (cols, hidden)).T
     for i in range(scaled.shape[0]):
-        normed = (scaled[i] * gain_ref[...] + bias_ref[...]).astype(BF16)
+        normed = (scaled[i] * gain + bias).astype(BF16)
         update = contract(normed, w, 0, 0)
         out_ref[i] = (g_ref[i].astype(F32) * update).astype(BF16)
 
@@ -98,7 +110,7 @@
         rows, cols, chans = z.shape
         hidden = w_out.shape[0]
         each = hidden // parts
-        step = min(16, rows)
+        step = min(32, rows)
         gain_row = ln_gain.reshape(1, chans)
         bias_row = ln_bias.reshape(1, chans)
         par = pltpu.CompilerParams(dimension_semantics=("arbitrary",))
@@ -139,23 +151,23 @@
             name="triangle",
         )(mine)
         tri = lax.all_to_all(sums, axes, 0, 0, tiled=True).reshape(hidden, rows, cols)
-        gain_wide = jnp.broadcast_to(out_gain.reshape(hidden, 1), (hidden, cols))
-        bias_wide = jnp.broadcast_to(out_bias.reshape(hidden, 1), (hidden, cols))
+        gain_out = out_gain.reshape(1, hidden)
+        bias_out = out_bias.reshape(1, hidden)
         return pl.pallas_call(
             out_kernel,
             grid=(rows // step,),
             in_specs=[
                 pl.BlockSpec((hidden, step, cols), lambda i: (0, i, 0)),
                 z_spec,
-                whole_spec(gain_wide),
-                whole_spec(bias_wide),
+                whole_spec(gain_out),
+                whole_spec(bias_out),
                 whole_spec(w_out),
             ],
             out_specs=z_spec,
             out_shape=jax.ShapeDtypeStruct((rows, cols, chans), BF16),
             compiler_params=par,
             name="update",
-        )(tri, out_gate, gain_wide, bias_wide, w_out)
+        )(tri, out_gate, gain_out, bias_out, w_out)
 
     return body
 

time: 177 us -> 175 us (0.989)
  Pallas kernels: 27.6 us -> 25.7 us
where the time goes in v2:
time: 175 us
  blocking collectives  101 us (58%)
  waiting for transfers between devices  43.1 us (25%)
  Pallas kernels  25.7 us (15%)
  starting transfers between devices  3.67 us (2%)
    all_to_all x1, blocking collectives, body(): mine = lax.all_to_all(edges, axes, 0, 0, tiled=True)  101 us
    all_to_all x1, waiting for transfers between devices, body(): lax.all_to_all(sums, axes, 0, 0, tiled=True).reshape(hidden, rows, cols)  43.1 us
    pallas_call x1, Pallas kernels, body(): pl.pallas_call(edge_kernel, grid=(rows // step,), in_specs=[z_spec, pl.Bl...  9.07 us
    pallas_call x1, Pallas kernels, body(): pl.pallas_call(out_kernel, grid=(rows // step,), in_specs=[pl.BlockSpec((...  5.92 us
    pallas_call x1, Pallas kernels, body(): pl.pallas_call(gate_kernel, grid=(rows // step,), in_specs=[z_spec, whole...  5.62 us
    pallas_call x1, Pallas kernels, body(): pl.pallas_call(make_triangle_kernel(row_parts, col_parts), grid=(each,),...  5.07 us
    all_to_all x1, starting transfers between devices, body(): lax.all_to_all(sums, axes, 0, 0, tiled=True).reshape(hidden, rows, cols)  3.67 us
  transfers between devices with their start and end apart: 1, of which 1 were waited for; matrix products, arithmetic and copies ran while one was open for 0% of the time, Pallas kernels for 3%

profile of v2, /device:TPU:0, one launch (start us, length us, event | category | flops | bytes accessed | tf_op | source)
XLA Modules:
  0.0 174.8 jit_solution(3688738235495012454)
XLA Ops:
  0.0 9.1 %edges.1 = bf16[32,2,4,64,128]{4,3,2,1,0:T(8,128)(2,1)} custom-call(bf16[64,128,128]{2,1,0:T(8,128)(2,1)} %z_ref.3, s32[64,128]{1,0:T(8,128)} %m_ref.1, f32[1,128]{1,0:T(1,128)} %bitcast.6, f32[1,128]{1,0:T(1,128)} %bitcast.8, bf16[128,256]{1,0:T(8,128)(2,1)} %wp_ref.1, bf16[128,256]{1,0:T(8,128)(2,1)} %wg_ref.1), custom_call_target="tpu_custom_call" | custom-call | tf_op jit(solution)/shard_map/edges/pallas_call | solution.py:118
  9.1 101.1 %all_to_all.10.e_ref = bf16[32,2,4,64,128]{4,3,2,1,0:T(8,128)(2,1)} all-to-all(bf16[32,2,4,64,128]{4,3,2,1,0:T(8,128)(2,1)} %edges.1), channel_id=1, replica_groups=mesh['rows'=8,'ka'=4] {'rows','ka'}, dimensions={0} | all-to-all | bytes 8388608 | tf_op jit(solution)/shard_map/all_to_all | solution.py:134
  110.1 5.1 %triangle.1 = bf16[32,4,64,128]{3,2,1,0:T(8,128)(2,1)} custom-call(bf16[32,2,4,64,128]{4,3,2,1,0:T(8,128)(2,1)} %all_to_all.10.e_ref), custom_call_target="tpu_custom_call" | custom-call | tf_op jit(solution)/shard_map/triangle/pallas_call | solution.py:144
  115.2 3.7 %all-to-all-start.1 = ((bf16[32,4,64,128]{3,2,1,0:T(8,128)(2,1)}), bf16[32,4,64,128]{3,2,1,0:T(8,128)(2,1)S(1)}, u32[]{:S(2)}, u32[]{:S(2)}) async-start(bf16[32,4,64,128]{3,2,1,0:T(8,128)(2,1)} %triangle.1), calls=%async_computation.1 | async-start | bytes 4194304 | tf_op jit(solution)/shard_map/all_to_all | solution.py:153
  118.9 5.6 %out_gate.1.g_ref = bf16[64,128,128]{2,1,0:T(8,128)(2,1)} custom-call(bf16[64,128,128]{2,1,0:T(8,128)(2,1)} %z_ref.3, f32[1,128]{1,0:T(1,128)} %bitcast.7, f32[1,128]{1,0:T(1,128)} %bitcast.9, bf16[128,128]{1,0:T(8,128)(2,1)} %w_ref.2), custom_call_target="tpu_custom_call" | custom-call | tf_op jit(solution)/shard_map/out_gate/pallas_call | solution.py:135
  124.5 43.1 %all-to-all-done.1 = bf16[32,4,64,128]{3,2,1,0:T(8,128)(2,1)S(1)} async-done(((bf16[32,4,64,128]{3,2,1,0:T(8,128)(2,1)}), bf16[32,4,64,128]{3,2,1,0:T(8,128)(2,1)S(1)}, u32[]{:S(2)}, u32[]{:S(2)}) %all-to-all-start.1) | async-done | bytes 2097184 | tf_op jit(solution)/shard_map/all_to_all | solution.py:153
  167.6 0.0 copy-start
  167.6 1.3 copy-done
  168.9 5.9 %update.1 = bf16[64,128,128]{2,1,0:T(8,128)(2,1)} custom-call(bf16[128,64,128]{2,1,0:T(8,128)(2,1)} %bitcast.5, bf16[64,128,128]{2,1,0:T(8,128)(2,1)} %out_gate.1.g_ref, f32[1,128]{1,0:T(1,128)} %bitcast.10, f32[1,128]{1,0:T(1,128)} %bitcast.11, bf16[128,128]{1,0:T(8,128)(2,1)} %w_ref.3), custom_call_target="tpu_custom_call" | custom-call | tf_op jit(solution)/shard_map/update/pallas_call | solution.py:156
Async XLA Ops:
  115.2 52.4 %all-to-all-start.1 = ((bf16[32,4,64,128]{3,2,1,0:T(8,128)(2,1)}), bf16[32,4,64,128]{3,2,1,0:T(8,128)(2,1)S(1)}, u32[]{:S(2)}, u32[]{:S(2)}) async-start(bf16[32,4,64,128]{3,2,1,0:T(8,128)(2,1)} %triangle.1), calls=%async_computation.1 | async-start | bytes 4194304 | tf_op jit(solution)/shard_map/all_to_all | solution.py:153
  167.6 1.3 copy-start
